TPU v7x, 32 devices: a whole 2x2x4 slice. The times are simulated.
32 devices in a mesh: dp: 16 (over z, y, core), mp: 2 (over x).
Axes of the slice: x: 2, y: 2, z: 4, core: 2. Of those that a mesh axis runs over, the one named last changes fastest.
Arguments:
- inputs: bfloat16 [65536, 1024], P(('dp', 'mp')), may hold values from -6 to 6
- rand_blocks: int32 [16, 16, 62, 3], P('dp', 'mp'), may hold values from 1 to 62
- ln1_gain: float32 [1024], replicated, may hold values from 0.1 to 1.9
- ln1_bias: float32 [1024], replicated, may hold values from -4 to 4
- w_qkv: bfloat16 [3, 1024, 1024], P(None, None, 'mp'), may hold values from -0.1875 to 0.1875
- w_out: bfloat16 [1024, 1024], P('mp'), may hold values from -1.5 to 1.5
- ln2_gain: float32 [1024], replicated, may hold values from 0.1 to 1.9
- ln2_bias: float32 [1024], replicated, may hold values from -4 to 4
- w_up: bfloat16 [1024, 4096], P(None, 'mp'), may hold values from -0.1875 to 0.1875
- b_up: float32 [4096], P('mp'), may hold values from -6 to 6
- w_down: bfloat16 [4096, 1024], P('mp'), may hold values from -0.09375 to 0.09375
- b_down: float32 [1024], replicated, may hold values from -6 to 6
- cotangent: bfloat16 [65536, 1024], P(('dp', 'mp')), may hold values from -6 to 6
Outputs:
- output: float32 [65536, 1024], P(('dp', 'mp'))
- input_grad: float32 [65536, 1024], P(('dp', 'mp'))
- d_ln1_gain: float32 [1024], replicated
- d_ln1_bias: float32 [1024], replicated
- d_w_qkv: float32 [3, 1024, 1024], P(None, None, 'mp')
- d_w_out: float32 [1024, 1024], P('mp')
- d_ln2_gain: float32 [1024], replicated
- d_ln2_bias: float32 [1024], replicated
- d_w_up: float32 [1024, 4096], P(None, 'mp')
- d_b_up: float32 [4096], P('mp')
- d_w_down: float32 [4096, 1024], P('mp')
- d_b_down: float32 [1024], replicated
Inputs may be any that keep to these rules, and one draw needn't show every extreme that they name: `rand_blocks`: a block may appear more than once in a list and may equal a window or global block.
All inputs are finite; a program needn't handle non-finite values.
Results may differ from a plain program's by a relative error of at most 0.02.
Values may be sent and summed in bfloat16 or wider, within the bound.
A program may use at most 320 MiB of HBM per device.

v0:
```python
from functools import partial
import jax
import jax.numpy as jnp
from jax import lax
from jax.sharding import PartitionSpec as P

BLOCK = 64
EPSILON = 1e-05
PLAIN = (((1,), (1,)), ((), ()))
ROWWISE = (((0,), (0,)), ((), ()))
HIGH = lax.Precision.HIGHEST


def norm_rows(values, scale_vec, offset):
    centered = values - jnp.mean(values, axis=-1, keepdims=True)
    inv_std = lax.rsqrt(jnp.mean(centered * centered, axis=-1, keepdims=True) + EPSILON)
    normed = centered * inv_std
    return (normed * scale_vec + offset, normed, inv_std)


def norm_back(normed, inv_std, scale_vec, gradient):
    scaled = gradient * scale_vec
    inner_term = (
        scaled
        - jnp.mean(scaled, axis=-1, keepdims=True)
        - normed * jnp.mean(scaled * normed, axis=-1, keepdims=True)
    )
    return (inv_std * inner_term, jnp.sum(gradient * normed, 0), jnp.sum(gradient, 0))


def gelu_tanh(values):
    return jax.nn.gelu(values, approximate=True)


def block_table(random_rows, num_blocks):
    rows_idx = jnp.arange(num_blocks, dtype=jnp.int32)[:, None]
    steps_off = jnp.arange(-1, 2, dtype=jnp.int32)[None, :]
    window = jnp.clip(rows_idx + steps_off, 0, num_blocks - 1)
    filler = jnp.zeros((1, random_rows.shape[1]), jnp.int32)
    chosen = jnp.concatenate([filler, random_rows, filler], 0)
    first_cols = jnp.zeros((num_blocks, 1), jnp.int32)
    last_cols = first_cols + (num_blocks - 1)
    return jnp.concatenate([first_cols, last_cols, window, chosen], 1)


def make_selector(table_grp, num_blocks):
    flat_table = table_grp.reshape(-1)
    return (flat_table[:, None] == jnp.arange(num_blocks, dtype=jnp.int32)[None, :]).astype(
        jnp.bfloat16
    )


def pick_blocks(selector, both_flat, per_query, block_rows, head_width):
    picked = jnp.dot(selector, both_flat, preferred_element_type=jnp.float32).astype(jnp.bfloat16)
    picked = picked.reshape(8, per_query, 2, block_rows, head_width)
    key_grp = picked[:, :, 0].reshape(8, per_query * block_rows, head_width)
    value_grp = picked[:, :, 1].reshape(8, per_query * block_rows, head_width)
    return (key_grp, value_grp)


def attend_item(operands):
    query, keys, values, table = operands
    num_blocks, per_query = table.shape
    seq_len, head_width = query.shape
    block_rows = seq_len // num_blocks
    scaling = head_width ** (-0.5)
    both_flat = jnp.stack(
        [
            keys.reshape(num_blocks, block_rows * head_width),
            values.reshape(num_blocks, block_rows * head_width),
        ],
        1,
    ).reshape(num_blocks, 2 * block_rows * head_width)
    query_groups = query.reshape(num_blocks // 8, 8, block_rows, head_width)
    table_groups = table.reshape(num_blocks // 8, 8, per_query)

    def group_scores(group_ops):
        query_grp, table_grp = group_ops
        selector = make_selector(table_grp, num_blocks)
        key_grp, value_grp = pick_blocks(selector, both_flat, per_query, block_rows, head_width)
        scores = (
            jnp.einsum("nqd,nkd->nqk", query_grp, key_grp, preferred_element_type=jnp.float32)
            * scaling
        )
        highest = jnp.max(scores, axis=-1, keepdims=True)
        shifted = jnp.exp(scores - highest)
        totals = jnp.sum(shifted, axis=-1, keepdims=True)
        weights_low = (shifted / totals).astype(jnp.bfloat16)
        mixed_grp = jnp.einsum(
            "nqk,nkd->nqd", weights_low, value_grp, preferred_element_type=jnp.float32
        )
        return (mixed_grp, (highest + jnp.log(totals))[..., 0])

    mixed, sparse_log = lax.map(group_scores, (query_groups, table_groups))
    mixed = mixed.reshape(seq_len, head_width)
    end_rows = jnp.concatenate([query[:block_rows], query[seq_len - block_rows :]], 0)
    glob_scores = (
        lax.dot_general(end_rows, keys, PLAIN, preferred_element_type=jnp.float32) * scaling
    )
    glob_high = jnp.max(glob_scores, axis=-1, keepdims=True)
    glob_exp = jnp.exp(glob_scores - glob_high)
    glob_total = jnp.sum(glob_exp, axis=-1, keepdims=True)
    glob_mixed = jnp.dot(
        (glob_exp / glob_total).astype(jnp.bfloat16), values, preferred_element_type=jnp.float32
    )
    mixed = mixed.at[:block_rows].set(glob_mixed[:block_rows])
    mixed = mixed.at[seq_len - block_rows :].set(glob_mixed[block_rows:])
    return (mixed.astype(jnp.bfloat16), sparse_log, (glob_high + jnp.log(glob_total))[:, 0])


def attend_back(operands):
    query, keys, values, table, out_grad, sparse_log, glob_log = operands
    num_blocks, per_query = table.shape
    seq_len, head_width = query.shape
    block_rows = seq_len // num_blocks
    scaling = head_width ** (-0.5)
    both_flat = jnp.stack(
        [
            keys.reshape(num_blocks, block_rows * head_width),
            values.reshape(num_blocks, block_rows * head_width),
        ],
        1,
    ).reshape(num_blocks, 2 * block_rows * head_width)
    query_groups = query.reshape(num_blocks // 8, 8, block_rows, head_width)
    table_groups = table.reshape(num_blocks // 8, 8, per_query)
    inner_blocks = jnp.arange(num_blocks) % (num_blocks - 1) != 0
    grad_blocks = out_grad.reshape(num_blocks, block_rows, head_width)
    grad_blocks = jnp.where(inner_blocks[:, None, None], grad_blocks, jnp.zeros_like(grad_blocks))
    grad_groups = grad_blocks.reshape(num_blocks // 8, 8, block_rows, head_width)

    def group_back(carry, group_ops):
        query_grp, table_grp, grad_grp, log_grp = group_ops
        selector = make_selector(table_grp, num_blocks)
        key_grp, value_grp = pick_blocks(selector, both_flat, per_query, block_rows, head_width)
        scores = (
            jnp.einsum("nqd,nkd->nqk", query_grp, key_grp, preferred_element_type=jnp.float32)
            * scaling
        )
        probs = jnp.exp(scores - log_grp[..., None])
        prob_grad = jnp.einsum(
            "nqd,nkd->nqk", grad_grp, value_grp, preferred_element_type=jnp.float32
        )
        inner_sum = jnp.sum(probs * prob_grad, axis=-1, keepdims=True)
        score_grad = (probs * (prob_grad - inner_sum)).astype(jnp.bfloat16)
        query_grad = (
            jnp.einsum("nqk,nkd->nqd", score_grad, key_grp, preferred_element_type=jnp.float32)
            * scaling
        )
        key_part = (
            jnp.einsum("nqk,nqd->nkd", score_grad, query_grp, preferred_element_type=jnp.float32)
            * scaling
        )
        value_part = jnp.einsum(
            "nqk,nqd->nkd", probs.astype(jnp.bfloat16), grad_grp, preferred_element_type=jnp.float32
        )
        parts = jnp.stack(
            [
                key_part.reshape(8 * per_query, block_rows * head_width),
                value_part.reshape(8 * per_query, block_rows * head_width),
            ],
            1,
        )
        parts = parts.reshape(8 * per_query, 2 * block_rows * head_width)
        carry = carry + lax.dot_general(
            selector.astype(jnp.float32),
            parts,
            ROWWISE,
            precision=HIGH,
            preferred_element_type=jnp.float32,
        )
        return (carry, query_grad)

    zero_blocks = jnp.zeros((num_blocks, 2 * block_rows * head_width), jnp.float32)
    accum, query_grad = lax.scan(
        group_back, zero_blocks, (query_groups, table_groups, grad_groups, sparse_log)
    )
    accum = accum.reshape(num_blocks, 2, block_rows, head_width)
    key_acc = accum[:, 0].reshape(seq_len, head_width)
    value_acc = accum[:, 1].reshape(seq_len, head_width)
    query_grad = query_grad.reshape(seq_len, head_width)
    end_rows = jnp.concatenate([query[:block_rows], query[seq_len - block_rows :]], 0)
    end_grad = jnp.concatenate([out_grad[:block_rows], out_grad[seq_len - block_rows :]], 0)
    glob_scores = (
        lax.dot_general(end_rows, keys, PLAIN, preferred_element_type=jnp.float32) * scaling
    )
    glob_probs = jnp.exp(glob_scores - glob_log[:, None])
    glob_pgrad = lax.dot_general(end_grad, values, PLAIN, preferred_element_type=jnp.float32)
    glob_inner = jnp.sum(glob_probs * glob_pgrad, axis=-1, keepdims=True)
    glob_sgrad = (glob_probs * (glob_pgrad - glob_inner)).astype(jnp.bfloat16)
    glob_qgrad = jnp.dot(glob_sgrad, keys, preferred_element_type=jnp.float32) * scaling
    query_grad = query_grad.at[:block_rows].add(glob_qgrad[:block_rows])
    query_grad = query_grad.at[seq_len - block_rows :].add(glob_qgrad[block_rows:])
    key_grad = (
        key_acc
        + lax.dot_general(glob_sgrad, end_rows, ROWWISE, preferred_element_type=jnp.float32)
        * scaling
    )
    value_grad = value_acc + lax.dot_general(
        glob_probs.astype(jnp.bfloat16), end_grad, ROWWISE, preferred_element_type=jnp.float32
    )
    return (query_grad, key_grad, value_grad)


def per_device(
    inputs,
    rand_blocks,
    ln1_gain,
    ln1_bias,
    w_qkv,
    w_out,
    ln2_gain,
    ln2_bias,
    w_up,
    b_up,
    w_down,
    b_down,
    cotangent,
):
    seqs_here = rand_blocks.shape[0]
    heads_here = rand_blocks.shape[1]
    item_count = seqs_here * heads_here
    head_width = w_qkv.shape[2] // heads_here
    residual_in = inputs.astype(jnp.float32)
    normed_one, normed_a, inv_a = norm_rows(residual_in, ln1_gain, ln1_bias)
    first_rows = lax.all_gather(normed_one.astype(jnp.bfloat16), "mp", axis=0, tiled=True)
    group_rows = first_rows.shape[0]
    seq_len = group_rows // seqs_here
    num_blocks = seq_len // BLOCK
    projected = jnp.einsum(
        "td,cde->cte", first_rows, w_qkv, preferred_element_type=jnp.float32
    ).astype(jnp.bfloat16)
    heads_qkv = projected.reshape(3, seqs_here, seq_len, heads_here, head_width).transpose(
        0, 1, 3, 2, 4
    )
    heads_qkv = heads_qkv.reshape(3, item_count, seq_len, head_width)
    tables = jax.vmap(partial(block_table, num_blocks=num_blocks))(
        rand_blocks.reshape(item_count, num_blocks - 2, rand_blocks.shape[3])
    )
    mixed, sparse_log, glob_log = lax.map(
        attend_item, (heads_qkv[0], heads_qkv[1], heads_qkv[2], tables)
    )
    attn_mix = (
        mixed.reshape(seqs_here, heads_here, seq_len, head_width)
        .transpose(0, 2, 1, 3)
        .reshape(group_rows, heads_here * head_width)
    )
    attn_out = lax.psum_scatter(
        jnp.dot(attn_mix, w_out, preferred_element_type=jnp.float32).astype(jnp.bfloat16),
        "mp",
        scatter_dimension=0,
        tiled=True,
    ).astype(jnp.float32)
    mid_resid = residual_in + attn_out
    normed_two, normed_b, inv_b = norm_rows(mid_resid, ln2_gain, ln2_bias)
    second_rows, grad_rows = (
        lax.all_gather(normed_two.astype(jnp.bfloat16), "mp", axis=0, tiled=True),
        lax.all_gather(cotangent, "mp", axis=0, tiled=True),
    )
    hidden_pre = jnp.dot(second_rows, w_up, preferred_element_type=jnp.float32) + b_up
    hidden_act = gelu_tanh(hidden_pre).astype(jnp.bfloat16)
    branch_out = lax.psum_scatter(
        jnp.dot(hidden_act, w_down, preferred_element_type=jnp.float32).astype(jnp.bfloat16),
        "mp",
        scatter_dimension=0,
        tiled=True,
    ).astype(jnp.float32)
    result = mid_resid + (branch_out + b_down)
    grad_own = cotangent.astype(jnp.float32)
    bias_down_grad = jnp.sum(grad_own, 0)
    down_grad = lax.dot_general(hidden_act, grad_rows, ROWWISE, preferred_element_type=jnp.float32)
    act_grad = lax.dot_general(grad_rows, w_down, PLAIN, preferred_element_type=jnp.float32)
    gelu_pull = jax.vjp(gelu_tanh, hidden_pre)[1]
    pre_grad = gelu_pull(act_grad)[0].astype(jnp.bfloat16)
    bias_up_grad = jnp.sum(pre_grad.astype(jnp.float32), 0)
    up_grad = lax.dot_general(second_rows, pre_grad, ROWWISE, preferred_element_type=jnp.float32)
    second_grad = lax.psum_scatter(
        lax.dot_general(pre_grad, w_up, PLAIN, preferred_element_type=jnp.float32).astype(
            jnp.bfloat16
        ),
        "mp",
        scatter_dimension=0,
        tiled=True,
    ).astype(jnp.float32)
    mid_part, gain_two_grad, bias_two_grad = norm_back(normed_b, inv_b, ln2_gain, second_grad)
    mid_grad = grad_own + mid_part
    attn_grad_rows = lax.all_gather(mid_grad.astype(jnp.bfloat16), "mp", axis=0, tiled=True)
    out_grad = lax.dot_general(
        attn_mix, attn_grad_rows, ROWWISE, preferred_element_type=jnp.float32
    )
    mix_grad = lax.dot_general(
        attn_grad_rows, w_out, PLAIN, preferred_element_type=jnp.float32
    ).astype(jnp.bfloat16)
    mix_items = (
        mix_grad.reshape(seqs_here, seq_len, heads_here, head_width)
        .transpose(0, 2, 1, 3)
        .reshape(item_count, seq_len, head_width)
    )
    query_grads, key_grads, value_grads = lax.map(
        attend_back,
        (heads_qkv[0], heads_qkv[1], heads_qkv[2], tables, mix_items, sparse_log, glob_log),
    )
    stacked = jnp.stack([query_grads, key_grads, value_grads]).astype(jnp.bfloat16)
    stacked = (
        stacked.reshape(3, seqs_here, heads_here, seq_len, head_width)
        .transpose(0, 1, 3, 2, 4)
        .reshape(3, group_rows, heads_here * head_width)
    )
    qkv_grad = jnp.einsum("td,cte->cde", first_rows, stacked, preferred_element_type=jnp.float32)
    first_grad = lax.psum_scatter(
        jnp.einsum("cte,cde->td", stacked, w_qkv, preferred_element_type=jnp.float32).astype(
            jnp.bfloat16
        ),
        "mp",
        scatter_dimension=0,
        tiled=True,
    ).astype(jnp.float32)
    input_part, gain_one_grad, bias_one_grad = norm_back(normed_a, inv_a, ln1_gain, first_grad)
    input_grad = mid_grad + input_part
    small_sums = lax.psum(
        (gain_one_grad, bias_one_grad, gain_two_grad, bias_two_grad, bias_down_grad), ("dp", "mp")
    )
    qkv_grad, out_grad, up_grad, bias_up_grad, down_grad = (
        lax.psum(qkv_grad.astype(jnp.bfloat16), "dp").astype(jnp.float32),
        lax.psum(out_grad.astype(jnp.bfloat16), "dp").astype(jnp.float32),
        lax.psum(up_grad.astype(jnp.bfloat16), "dp").astype(jnp.float32),
        lax.psum(bias_up_grad.astype(jnp.bfloat16), "dp").astype(jnp.float32),
        lax.psum(down_grad.astype(jnp.bfloat16), "dp").astype(jnp.float32),
    )
    return (
        result,
        input_grad,
        small_sums[0],
        small_sums[1],
        qkv_grad,
        out_grad,
        small_sums[2],
        small_sums[3],
        up_grad,
        bias_up_grad,
        down_grad,
        small_sums[4],
    )


def solution(mesh):
    return jax.shard_map(
        per_device,
        mesh=mesh,
        in_specs=(
            P(("dp", "mp"), None),
            P("dp", "mp", None, None),
            P(),
            P(),
            P(None, None, "mp"),
            P("mp", None),
            P(),
            P(),
            P(None, "mp"),
            P("mp"),
            P("mp", None),
            P(),
            P(("dp", "mp"), None),
        ),
        out_specs=(
            P(("dp", "mp"), None),
            P(("dp", "mp"), None),
            P(),
            P(),
            P(None, None, "mp"),
            P("mp", None),
            P(),
            P(),
            P(None, "mp"),
            P("mp"),
            P("mp", None),
            P(),
        ),
        check_vma=False,
    )
```

profile of v0, /device:TPU:0, one launch (start us, length us, event | category | flops | bytes accessed | tf_op | source)
XLA Modules:
  0.0 5234.4 jit_solution(17163692770296250939)
XLA Ops:
  17.8 106.0 %all-gather.5.cloned.1.call-done = bf16[4096,1024]{1,0:T(8,128)(2,1)} async-done(((bf16[2048,1024]{1,0:T(8,128)(2,1)}), bf16[4096,1024]{1,0:T(8,128)(2,1)}) %all-gather.5.cloned.1.call-update) | async-done | bytes 8388624 | tf_op jit(solution)/shard_map/all_gather | solution.py:225
  123.9 19.1 convolution_convert_fusion.2
  143.0 22.8 copy.97
  165.9 16.7 slice_bitcast_fusion
  182.6 964.2 %while.96 = (s32[]{:T(128)}, bf16[8,4096,64]{1,2,0:T(8,128)(2,1)}, f32[8,8,8,64]{3,2,1,0:T(8,128)}, f32[8,128]{1,0:T(8,128)}, bf16[8,4096,64]{2,1,0:T(8,128)(2,1...) while((s32[]{:T(128)}, bf16[8,4096,64]{1,2,0:T(8,128)(2,1)}, ...), condition=%wide.region_9.10_spmd, body=%wide.region_2.9_spmd.sunk | while | flops 275025280 | bytes 29968956 | solution.py:239
  200.6 93.5 %while.99 = (s32[]{:T(128)}, bf16[8,8,64,64]{3,2,1,0:T(8,128)(2,1)}, f32[8,8,64]{2,1,0:T(8,128)S(1)}, bf16[8,8,64,64]{3,2,1,0:T(8,128)(2,1)}, s32[8,8,8]{2,1,0:T...) while((s32[]{:T(128)}, bf16[8,8,64,64]{3,2,1,0:T(8,128)(2,1)}, f32[8,8,64]{2,1,0:T(8,128)S(1)}, ...), condition=%wide.region_6.6_spmd, body=%wide.region_3.5_spmd.sunk | while | flops 136580608 | bytes 10903893 | solution.py:94
  321.1 93.5 %while.99 = (s32[]{:T(128)}, bf16[8,8,64,64]{3,2,1,0:T(8,128)(2,1)}, f32[8,8,64]{2,1,0:T(8,128)S(1)}, bf16[8,8,64,64]{3,2,1,0:T(8,128)(2,1)}, s32[8,8,8]{2,1,0:T...) while((s32[]{:T(128)}, bf16[8,8,64,64]{3,2,1,0:T(8,128)(2,1)}, f32[8,8,64]{2,1,0:T(8,128)S(1)}, ...), condition=%wide.region_6.6_spmd, body=%wide.region_3.5_spmd.sunk | while | flops 136580608 | bytes 10903893 | solution.py:94
  441.6 93.5 %while.99 = (s32[]{:T(128)}, bf16[8,8,64,64]{3,2,1,0:T(8,128)(2,1)}, f32[8,8,64]{2,1,0:T(8,128)S(1)}, bf16[8,8,64,64]{3,2,1,0:T(8,128)(2,1)}, s32[8,8,8]{2,1,0:T...) while((s32[]{:T(128)}, bf16[8,8,64,64]{3,2,1,0:T(8,128)(2,1)}, f32[8,8,64]{2,1,0:T(8,128)S(1)}, ...), condition=%wide.region_6.6_spmd, body=%wide.region_3.5_spmd.sunk | while | flops 136580608 | bytes 10903893 | solution.py:94
  562.0 93.5 %while.99 = (s32[]{:T(128)}, bf16[8,8,64,64]{3,2,1,0:T(8,128)(2,1)}, f32[8,8,64]{2,1,0:T(8,128)S(1)}, bf16[8,8,64,64]{3,2,1,0:T(8,128)(2,1)}, s32[8,8,8]{2,1,0:T...) while((s32[]{:T(128)}, bf16[8,8,64,64]{3,2,1,0:T(8,128)(2,1)}, f32[8,8,64]{2,1,0:T(8,128)S(1)}, ...), condition=%wide.region_6.6_spmd, body=%wide.region_3.5_spmd.sunk | while | flops 136580608 | bytes 10903893 | solution.py:94
  682.5 93.5 %while.99 = (s32[]{:T(128)}, bf16[8,8,64,64]{3,2,1,0:T(8,128)(2,1)}, f32[8,8,64]{2,1,0:T(8,128)S(1)}, bf16[8,8,64,64]{3,2,1,0:T(8,128)(2,1)}, s32[8,8,8]{2,1,0:T...) while((s32[]{:T(128)}, bf16[8,8,64,64]{3,2,1,0:T(8,128)(2,1)}, f32[8,8,64]{2,1,0:T(8,128)S(1)}, ...), condition=%wide.region_6.6_spmd, body=%wide.region_3.5_spmd.sunk | while | flops 136580608 | bytes 10903893 | solution.py:94
  802.9 93.5 %while.99 = (s32[]{:T(128)}, bf16[8,8,64,64]{3,2,1,0:T(8,128)(2,1)}, f32[8,8,64]{2,1,0:T(8,128)S(1)}, bf16[8,8,64,64]{3,2,1,0:T(8,128)(2,1)}, s32[8,8,8]{2,1,0:T...) while((s32[]{:T(128)}, bf16[8,8,64,64]{3,2,1,0:T(8,128)(2,1)}, f32[8,8,64]{2,1,0:T(8,128)S(1)}, ...), condition=%wide.region_6.6_spmd, body=%wide.region_3.5_spmd.sunk | while | flops 136580608 | bytes 10903893 | solution.py:94
  923.4 93.5 %while.99 = (s32[]{:T(128)}, bf16[8,8,64,64]{3,2,1,0:T(8,128)(2,1)}, f32[8,8,64]{2,1,0:T(8,128)S(1)}, bf16[8,8,64,64]{3,2,1,0:T(8,128)(2,1)}, s32[8,8,8]{2,1,0:T...) while((s32[]{:T(128)}, bf16[8,8,64,64]{3,2,1,0:T(8,128)(2,1)}, f32[8,8,64]{2,1,0:T(8,128)S(1)}, ...), condition=%wide.region_6.6_spmd, body=%wide.region_3.5_spmd.sunk | while | flops 136580608 | bytes 10903893 | solution.py:94
  1043.8 93.5 %while.99 = (s32[]{:T(128)}, bf16[8,8,64,64]{3,2,1,0:T(8,128)(2,1)}, f32[8,8,64]{2,1,0:T(8,128)S(1)}, bf16[8,8,64,64]{3,2,1,0:T(8,128)(2,1)}, s32[8,8,8]{2,1,0:T...) while((s32[]{:T(128)}, bf16[8,8,64,64]{3,2,1,0:T(8,128)(2,1)}, f32[8,8,64]{2,1,0:T(8,128)S(1)}, ...), condition=%wide.region_6.6_spmd, body=%wide.region_3.5_spmd.sunk | while | flops 136580608 | bytes 10903893 | solution.py:94
  1146.8 10.5 convolution_convert_fusion.5
  1157.5 99.4 %reduce-scatter.5.cloned.1.call-done = bf16[2048,1024]{1,0:T(8,128)(2,1)} async-done(((bf16[4096,1024]{1,0:T(8,128)(2,1)}), bf16[2048,1024]{1,0:T(8,128)(2,1)}) %reduce-scatter.5.cloned.1.call-update) | async-done | bytes 4194320 | tf_op jit(solution)/shard_map/reduce_scatter | solution.py:247
  1269.3 103.5 %all-gather.7.cloned.1.call-done = bf16[4096,1024]{1,0:T(8,128)(2,1)} async-done(((bf16[2048,1024]{1,0:T(8,128)(2,1)}), bf16[4096,1024]{1,0:T(8,128)(2,1)}) %all-gather.7.cloned.1.call-update) | async-done | bytes 8388624 | tf_op jit(solution)/shard_map/all_gather | solution.py:256
  1372.8 34.0 multiply_convert_fusion.2
  1406.8 71.4 %all-gather.9.cloned.1.call-done = bf16[4096,1024]{1,0:T(8,128)(2,1)} async-done(((bf16[2048,1024]{1,0:T(8,128)(2,1)}), bf16[4096,1024]{1,0:T(8,128)(2,1)}) %all-gather.9.cloned.1.call-update) | async-done | bytes 8388624 | tf_op jit(solution)/shard_map/all_gather | solution.py:257
  1478.2 45.3 fusion.101
  1523.6 23.8 convolution_convert_fusion.3
  1547.4 99.4 %reduce-scatter.9.cloned.1.call-done = bf16[2048,1024]{1,0:T(8,128)(2,1)} async-done(((bf16[4096,1024]{1,0:T(8,128)(2,1)}), bf16[2048,1024]{1,0:T(8,128)(2,1)}) %reduce-scatter.9.cloned.1.call-update) | async-done | bytes 4194320 | tf_op jit(solution)/shard_map/reduce_scatter | solution.py:276
  1646.8 9.1 fusion.86
  1656.5 7.1 fusion.94
  1663.8 24.3 convolution_convert_fusion.8
  1688.1 23.7 convolution_convert_fusion.7
  1711.8 56.0 %all-gather.11.cloned.1.call-done = bf16[4096,1024]{1,0:T(8,128)(2,1)} async-done(((bf16[2048,1024]{1,0:T(8,128)(2,1)}), bf16[4096,1024]{1,0:T(8,128)(2,1)}) %all-gather.11.cloned.1.call-update) | async-done | bytes 8388624 | tf_op jit(solution)/shard_map/all_gather | solution.py:286
  1767.9 10.1 convolution_convert_fusion.6
  1778.0 8.3 copy.100
  1786.3 2913.1 %while.98 = (s32[]{:T(128)}, bf16[8,4096,64]{1,2,0:T(8,128)(2,1)}, bf16[8,4096,64]{1,2,0:T(8,128)(2,1)}, bf16[8,4096,64]{1,2,0:T(8,128)(2,1)}, bf16[8,4096,64]{2...) while((s32[]{:T(128)}, bf16[8,4096,64]{1,2,0:T(8,128)(2,1)}, ...), condition=%wide.region_22.23_spmd, body=%wide.region_17.22_spmd.sunk | while | flops 983490496 | bytes 111270584 | solution.py:298
  1809.6 307.4 %while.100 = (s32[]{:T(128)}, f32[64,8192]{1,0:T(8,128)}, f32[8,8,64,64]{3,2,1,0:T(8,128)}, s32[8,8,8]{2,1,0:T(8,128)S(1)}, bf16[8,8,64,64]{3,2,1,0:T(8,128)(2,1...) while((s32[]{:T(128)}, f32[64,8192]{1,0:T(8,128)}, ...), condition=%wide.region_20.20_spmd.clone, body=%wide.region_18.19_spmd.clone.sunk | while | flops 642031104 | bytes 48511176 | solution.py:174
  2032.8 4.8 convolution_add_fusion.3
  2071.3 4.8 convolution_add_fusion.3
  2121.7 4.9 fusion.189
  2173.7 307.4 %while.100 = (s32[]{:T(128)}, f32[64,8192]{1,0:T(8,128)}, f32[8,8,64,64]{3,2,1,0:T(8,128)}, s32[8,8,8]{2,1,0:T(8,128)S(1)}, bf16[8,8,64,64]{3,2,1,0:T(8,128)(2,1...) while((s32[]{:T(128)}, f32[64,8192]{1,0:T(8,128)}, ...), condition=%wide.region_20.20_spmd.clone, body=%wide.region_18.19_spmd.clone.sunk | while | flops 642031104 | bytes 48511176 | solution.py:174
  2435.4 4.8 convolution_add_fusion.3
  2485.7 4.9 fusion.189
  2537.7 307.4 %while.100 = (s32[]{:T(128)}, f32[64,8192]{1,0:T(8,128)}, f32[8,8,64,64]{3,2,1,0:T(8,128)}, s32[8,8,8]{2,1,0:T(8,128)S(1)}, bf16[8,8,64,64]{3,2,1,0:T(8,128)(2,1...) while((s32[]{:T(128)}, f32[64,8192]{1,0:T(8,128)}, ...), condition=%wide.region_20.20_spmd.clone, body=%wide.region_18.19_spmd.clone.sunk | while | flops 642031104 | bytes 48511176 | solution.py:174
  2606.9 4.8 convolution_add_fusion.3
  2849.8 4.9 fusion.189
  2901.8 307.4 %while.100 = (s32[]{:T(128)}, f32[64,8192]{1,0:T(8,128)}, f32[8,8,64,64]{3,2,1,0:T(8,128)}, s32[8,8,8]{2,1,0:T(8,128)S(1)}, bf16[8,8,64,64]{3,2,1,0:T(8,128)(2,1...) while((s32[]{:T(128)}, f32[64,8192]{1,0:T(8,128)}, ...), condition=%wide.region_20.20_spmd.clone, body=%wide.region_18.19_spmd.clone.sunk | while | flops 642031104 | bytes 48511176 | solution.py:174
  3125.0 4.8 convolution_add_fusion.3
  3213.8 4.9 fusion.189
  3265.9 307.4 %while.100 = (s32[]{:T(128)}, f32[64,8192]{1,0:T(8,128)}, f32[8,8,64,64]{3,2,1,0:T(8,128)}, s32[8,8,8]{2,1,0:T(8,128)S(1)}, bf16[8,8,64,64]{3,2,1,0:T(8,128)(2,1...) while((s32[]{:T(128)}, f32[64,8192]{1,0:T(8,128)}, ...), condition=%wide.region_20.20_spmd.clone, body=%wide.region_18.19_spmd.clone.sunk | while | flops 642031104 | bytes 48511176 | solution.py:174
  3577.9 4.9 fusion.189
  3629.9 307.4 %while.100 = (s32[]{:T(128)}, f32[64,8192]{1,0:T(8,128)}, f32[8,8,64,64]{3,2,1,0:T(8,128)}, s32[8,8,8]{2,1,0:T(8,128)S(1)}, bf16[8,8,64,64]{3,2,1,0:T(8,128)(2,1...) while((s32[]{:T(128)}, f32[64,8192]{1,0:T(8,128)}, ...), condition=%wide.region_20.20_spmd.clone, body=%wide.region_18.19_spmd.clone.sunk | while | flops 642031104 | bytes 48511176 | solution.py:174
  3942.0 4.9 fusion.189
  3994.0 307.4 %while.100 = (s32[]{:T(128)}, f32[64,8192]{1,0:T(8,128)}, f32[8,8,64,64]{3,2,1,0:T(8,128)}, s32[8,8,8]{2,1,0:T(8,128)S(1)}, bf16[8,8,64,64]{3,2,1,0:T(8,128)(2,1...) while((s32[]{:T(128)}, f32[64,8192]{1,0:T(8,128)}, ...), condition=%wide.region_20.20_spmd.clone, body=%wide.region_18.19_spmd.clone.sunk | while | flops 642031104 | bytes 48511176 | solution.py:174
  4306.0 4.9 fusion.189
  4358.0 307.4 %while.100 = (s32[]{:T(128)}, f32[64,8192]{1,0:T(8,128)}, f32[8,8,64,64]{3,2,1,0:T(8,128)}, s32[8,8,8]{2,1,0:T(8,128)S(1)}, bf16[8,8,64,64]{3,2,1,0:T(8,128)(2,1...) while((s32[]{:T(128)}, f32[64,8192]{1,0:T(8,128)}, ...), condition=%wide.region_20.20_spmd.clone, body=%wide.region_18.19_spmd.clone.sunk | while | flops 642031104 | bytes 48511176 | solution.py:174
  4670.1 4.9 fusion.189
  4699.4 8.0 pad_maximum_fusion.6
  4707.5 11.5 convolution_convert_fusion.9
  4719.0 14.5 convert_bitcast_fusion.3
  4733.6 18.4 bitcast_convert_fusion
  4752.0 23.6 convolution_convert_fusion.4
  4776.3 34.9 psum.77
  4811.8 154.5 %all-reduce.4.cloned.1.call-done = (bf16[3,1024,512]{1,2,0:T(8,128)(2,1)}, bf16[512,1024]{1,0:T(8,128)(2,1)}, bf16[1024,2048]{1,0:T(8,128)(2,1)}, bf16[2048,1024]{1,0:T(8,128)(2,1)}) async-done(((bf16[3,1024,512]{1,2,0:T(8,128)(2,1)}, bf16[512,1024]{1,0:T(8,128)(2,1)}, bf16[1024,2048]{1,0:T(8,128)(2,1)}, bf16[2048,1024]{1,0:T(8,128)(2,1)}), (bf16[3,1024,512]{1,2,0:T(8,128)(2,1)}, ...) | async-done | bytes 12582928 | tf_op jit(solution)/shard_map/psum | solution.py:323
  4966.3 6.8 convert_element_type.164
  4977.7 5.5 copy.103
  4985.9 82.6 %reduce-scatter.11.cloned.1.call-done = bf16[2048,1024]{1,0:T(8,128)(2,1)} async-done(((bf16[4096,1024]{1,0:T(8,128)(2,1)}), bf16[2048,1024]{1,0:T(8,128)(2,1)}) %reduce-scatter.11.cloned.1.call-update) | async-done | bytes 4194320 | tf_op jit(solution)/shard_map/reduce_scatter | solution.py:309
  5068.5 6.1 fusion.87
  5074.7 96.1 %reduce-scatter.7.cloned.1.call-done = bf16[2048,1024]{1,0:T(8,128)(2,1)} async-done(((bf16[4096,1024]{1,0:T(8,128)(2,1)}), bf16[2048,1024]{1,0:T(8,128)(2,1)}) %reduce-scatter.7.cloned.1.call-update) | async-done | bytes 4194320 | tf_op jit(solution)/shard_map/reduce_scatter | solution.py:261
  5170.8 17.0 fusion.80
  5187.8 39.9 all-reduce
  (2685 shorter events, 3839.0 us)
Async XLA Ops:
  7.2 116.7 %copy-start = (bf16[3,1024,512]{2,1,0:T(8,128)(2,1)S(1)}, bf16[3,1024,512]{2,1,0:T(8,128)(2,1)}, u32[]{:S(2)}) copy-start(bf16[3,1024,512]{2,1,0:T(8,128)(2,1)} %param.33) | copy-start | bytes 9437188
  7.2 6.8 copy-start.33
  7.2 6.8 copy-start.38
  7.2 116.6 %all-gather.5.cloned.1.call-start = ((), (), s32[]{:S(2)}) async-start(), calls=%async_computation.4 | async-start | bytes 12582912 | tf_op jit(solution)/shard_map/all_gather | solution.py:225
  7.3 6.7 copy-start.5
  10.3 7.1 copy-start.37
  17.0 1239.9 %reduce-scatter.5.cloned.1.call-start = ((), (), s32[]{:S(2)}) async-start(), calls=%async_computation.5 | async-start | bytes 12582912 | tf_op jit(solution)/shard_map/reduce_scatter | solution.py:247
  1146.8 10.6 copy-start.15
  1157.4 107.8 %copy-start.30 = (f32[1024]{0:T(1024)S(1)}, f32[1024]{0:T(1024)}, u32[]{:S(2)}) copy-start(f32[1024]{0:T(1024)} %param.35) | copy-start | bytes 12292
  1157.4 107.8 %copy-start.39 = (f32[1024]{0:T(1024)S(1)}, f32[1024]{0:T(1024)}, u32[]{:S(2)}) copy-start(f32[1024]{0:T(1024)} %param.36) | copy-start | bytes 12292
  1157.4 215.4 %all-gather.7.cloned.1.call-start = ((), (), s32[]{:S(2)}) async-start(), calls=%async_computation.6 | async-start | bytes 12582912 | tf_op jit(solution)/shard_map/all_gather | solution.py:256
  1256.9 4.8 copy-start.6
  1256.9 5.9 copy-start.10
  1265.2 107.6 %copy-start.43 = (f32[2048]{0:T(1024)S(1)}, f32[2048]{0:T(1024)}, u32[]{:S(2)}) copy-start(f32[2048]{0:T(1024)} %param.38) | copy-start | bytes 24580
  1268.7 209.6 %all-gather.9.cloned.1.call-start = ((), (), s32[]{:S(2)}) async-start(), calls=%async_computation.8 | async-start | bytes 12582912 | tf_op jit(solution)/shard_map/all_gather | solution.py:257
  1269.3 377.5 %reduce-scatter.9.cloned.1.call-start = ((), (), s32[]{:S(2)}) async-start(), calls=%async_computation.9 | async-start | bytes 12582912 | tf_op jit(solution)/shard_map/reduce_scatter | solution.py:276
  1547.3 99.5 %copy-start.17 = (f32[2048]{0:T(1024)S(1)}, f32[2048]{0:T(1024)}, u32[]{:S(2)}) copy-start(f32[2048]{0:T(1024)} %copy-done.16) | copy-start | bytes 24580
  1547.3 99.5 %copy-start.22 = (f32[2048]{0:T(1024)S(1)}, f32[2048]{0:T(1024)}, u32[]{:S(2)}) copy-start(f32[2048]{0:T(1024)} %copy-done.21) | copy-start | bytes 24580
  1547.3 99.5 %copy-start.31 = (f32[1024]{0:T(1024)S(1)}, f32[1024]{0:T(1024)}, u32[]{:S(2)}) copy-start(f32[1024]{0:T(1024)} %param.35) | copy-start | bytes 12292
  1547.3 220.5 %all-gather.11.cloned.1.call-start = ((), (), s32[]{:S(2)}) async-start(), calls=%async_computation.10 | async-start | bytes 12582912 | tf_op jit(solution)/shard_map/all_gather | solution.py:286
  1646.8 9.7 copy-start.7
  1646.8 9.7 copy-start.11
  1646.8 9.7 copy-start.12
  1663.7 3302.6 %all-reduce.4.cloned.1.call-start = ((), (), s32[]{:S(2)}) async-start(), calls=%async_computation.12 | async-start | bytes 25165824 | tf_op jit(solution)/shard_map/psum | solution.py:323
  1818.4 3.3 copy-start.2
  1933.3 3.3 copy-start.2
  1971.8 3.3 copy-start.2
  2087.3 3.3 copy-start.2
  2182.4 3.3 copy-start.2
  2297.4 3.3 copy-start.2
  2451.3 3.3 copy-start.2
  2661.4 3.3 copy-start.2
  2815.4 3.3 copy-start.2
  2910.5 3.3 copy-start.2
  3025.5 3.3 copy-start.2
  3064.0 3.3 copy-start.2
  3179.4 3.3 copy-start.2
  3274.6 3.3 copy-start.2
  3389.5 3.3 copy-start.2
  3543.5 3.3 copy-start.2
  3753.6 3.3 copy-start.2
  3907.6 3.3 copy-start.2
  4117.6 3.3 copy-start.2
  4271.6 3.3 copy-start.2
  4481.7 3.3 copy-start.2
  4635.7 3.3 copy-start.2
  4699.4 8.0 copy-start.42
  4699.4 19.5 slice-start
  4707.4 11.5 copy-start.13
  4707.5 11.5 slice-start.1
  4733.5 335.0 %reduce-scatter.11.cloned.1.call-start = ((), (), s32[]{:S(2)}) async-start(), calls=%async_computation.11 | async-start | bytes 12582912 | tf_op jit(solution)/shard_map/reduce_scatter | solution.py:309
  4752.0 418.8 %reduce-scatter.7.cloned.1.call-start = ((), (), s32[]{:S(2)}) async-start(), calls=%async_computation.7 | async-start | bytes 12582912 | tf_op jit(solution)/shard_map/reduce_scatter | solution.py:261
  4966.3 6.8 copy-start.14
  4977.6 91.0 %copy-start.20 = (f32[2048]{0:T(1024)S(1)}, f32[2048]{0:T(1024)}, u32[]{:S(2)}) copy-start(f32[2048]{0:T(1024)} %copy-done.19) | copy-start | bytes 24580
  4977.6 91.0 %copy-start.25 = (f32[2048]{0:T(1024)S(1)}, f32[2048]{0:T(1024)}, u32[]{:S(2)}) copy-start(f32[2048]{0:T(1024)} %copy-done.24) | copy-start | bytes 24580
  4977.6 91.0 %copy-start.34 = (f32[1024]{0:T(1024)S(1)}, f32[1024]{0:T(1024)}, u32[]{:S(2)}) copy-start(f32[1024]{0:T(1024)} %param.31) | copy-start | bytes 12292
  4977.6 193.2 %copy-start.18 = (f32[2048]{0:T(1024)S(1)}, f32[2048]{0:T(1024)}, u32[]{:S(2)}) copy-start(f32[2048]{0:T(1024)} %copy-done.16) | copy-start | bytes 24580
  4977.6 193.2 %copy-start.23 = (f32[2048]{0:T(1024)S(1)}, f32[2048]{0:T(1024)}, u32[]{:S(2)}) copy-start(f32[2048]{0:T(1024)} %copy-done.21) | copy-start | bytes 24580
  4977.6 193.2 %copy-start.27 = (f32[2048]{0:T(1024)S(1)}, f32[2048]{0:T(1024)}, u32[]{:S(2)}) copy-start(f32[2048]{0:T(1024)} %copy-done.26) | copy-start | bytes 24580
  4977.6 193.2 %copy-start.29 = (f32[2048]{0:T(1024)S(1)}, f32[2048]{0:T(1024)}, u32[]{:S(2)}) copy-start(f32[2048]{0:T(1024)} %copy-done.28) | copy-start | bytes 24580
  4977.6 193.2 %copy-start.32 = (f32[1024]{0:T(1024)S(1)}, f32[1024]{0:T(1024)}, u32[]{:S(2)}) copy-start(f32[1024]{0:T(1024)} %param.35) | copy-start | bytes 12292
  4977.6 193.2 %copy-start.40 = (f32[1024]{0:T(1024)S(1)}, f32[1024]{0:T(1024)}, u32[]{:S(2)}) copy-start(f32[1024]{0:T(1024)} %param.40) | copy-start | bytes 12292
  5074.7 113.1 %copy-start.35 = (f32[1024]{0:T(1024)S(1)}, f32[1024]{0:T(1024)}, u32[]{:S(2)}) copy-start(f32[1024]{0:T(1024)} %get-tuple-element.546) | copy-start | bytes 12292
  5074.7 113.1 %copy-start.36 = (f32[1024]{0:T(1024)S(1)}, f32[1024]{0:T(1024)}, u32[]{:S(2)}) copy-start(f32[1024]{0:T(1024)} %get-tuple-element.552) | copy-start | bytes 12292
  (201 other events, 285.1 us)
Sparse Core Ops, SparseCore 0:
  17.1 106.6 all-gather.4
  1157.5 99.3 reduce-scatter.4
  1268.8 103.9 all-gather.6
  1374.2 103.9 all-gather.8
  1547.5 99.2 reduce-scatter.8
  1663.8 103.9 all-gather.10
  4733.6 232.6 all-reduce.3
  4969.1 99.3 reduce-scatter.10
  5071.4 99.3 reduce-scatter.6
where the time goes:
time: 5280 us; the launch traced here: 5230 us
  local copies, waits for them, and re-layouts  2110 us (40%)
  matrix products  1870 us (35%)
  waiting for transfers between devices  870 us (16%)
  other arithmetic  290 us (5%)
  blocking collectives  74.8 us (1%)
    reshape x128, local copies, waits for them, and re-layouts, pick_blocks(): picked = picked.reshape(8, per_query, 2, block_rows, head_width)  543 us
    reshape x128, local copies, waits for them, and re-layouts, group_back(): jnp.stack([key_part.reshape(8 * per_query, block_rows * head_width), valu...  373 us
    dot_general x128, matrix products, pick_blocks(): jnp.dot(selector, both_flat, preferred_element_type=jnp.float32)  344 us
    dot_general x64, matrix products, group_back(): lax.dot_general(selector.astype(jnp.float32), parts, ROWWISE, precision=H...  303 us
    mul x64, local copies, waits for them, and re-layouts, group_back(): jnp.einsum('nqk,nqd->nkd', score_grad, query_grp, preferred_element_type=...  207 us
    dot_general x64, matrix products, group_back(): jnp.einsum('nqk,nqd->nkd', probs.astype(jnp.bfloat16), grad_grp, preferre...  200 us
    psum x1, waiting for transfers between devices, per_device(): lax.psum(qkv_grad.astype(jnp.bfloat16), 'dp').astype(jnp.float32)  154 us
    dot_general x64, matrix products, group_back(): jnp.einsum('nqk,nkd->nqd', score_grad, key_grp, preferred_element_type=jn...  154 us
  transfers between devices with their start and end apart: 9, of which 9 were waited for; matrix products, arithmetic and copies ran while one was open for 3% of the time, Pallas kernels for 0%

commit v1 on v0

--- a/solution.py
+++ b/solution.py
@@ -320,7 +320,7 @@
         (gain_one_grad, bias_one_grad, gain_two_grad, bias_two_grad, bias_down_grad), ("dp", "mp")
     )
     qkv_grad, out_grad, up_grad, bias_up_grad, down_grad = (
-        lax.psum(qkv_grad.astype(jnp.bfloat16), "dp").astype(jnp.float32),
+        jnp.sum(lax.all_gather(qkv_grad.astype(jnp.bfloat16), "dp"), axis=0).astype(jnp.float32),
         lax.psum(out_grad.astype(jnp.bfloat16), "dp").astype(jnp.float32),
         lax.psum(up_grad.astype(jnp.bfloat16), "dp").astype(jnp.float32),
         lax.psum(bias_up_grad.astype(jnp.bfloat16), "dp").astype(jnp.float32),

time: 5280 us -> 5260 us (level)
    all_gather x0 -> x1, waiting for transfers between devices: none -> 189 us  [per_device(): lax.all_gather(qkv_grad.astype(jnp.bfloat16), 'dp')]
    psum x1, waiting for transfers between devices: 154 us -> 0.01 us  [per_device(): lax.psum(out_grad.astype(jnp.bfloat16), 'dp').astype(jnp.float32)]
    reduce_scatter x1, waiting for transfers between devices: 82.6 us -> 5.12 us  [per_device(): lax.psum_scatter(jnp.einsum('cte,cde->td', stacked, w_qkv, preferred_elem...]
  transfers between devices with their start and end apart: 9 -> 10, of which waited for: 9 -> 9; matrix products, arithmetic and copies ran while one was open for 3% -> 57% of each run, Pallas kernels for 0% -> 0%
where the time goes in v1:
time: 5260 us; the launch traced here: 5210 us
  local copies, waits for them, and re-layouts  2120 us (40%)
  matrix products  1870 us (36%)
  waiting for transfers between devices  826 us (16%)
  other arithmetic  307 us (6%)
  blocking collectives  75.6 us (1%)
    reshape x128, local copies, waits for them, and re-layouts, pick_blocks(): picked = picked.reshape(8, per_query, 2, block_rows, head_width)  543 us
    reshape x128, local copies, waits for them, and re-layouts, group_back(): jnp.stack([key_part.reshape(8 * per_query, block_rows * head_width), valu...  372 us
    dot_general x128, matrix products, pick_blocks(): jnp.dot(selector, both_flat, preferred_element_type=jnp.float32)  341 us
    dot_general x64, matrix products, group_back(): lax.dot_general(selector.astype(jnp.float32), parts, ROWWISE, precision=H...  303 us
    mul x64, local copies, waits for them, and re-layouts, group_back(): jnp.einsum('nqk,nqd->nkd', score_grad, query_grp, preferred_element_type=...  206 us
    dot_general x64, matrix products, group_back(): jnp.einsum('nqk,nqd->nkd', probs.astype(jnp.bfloat16), grad_grp, preferre...  200 us
    all_gather x1, waiting for transfers between devices, per_device(): lax.all_gather(qkv_grad.astype(jnp.bfloat16), 'dp')  189 us
    dot_general x64, matrix products, group_back(): jnp.einsum('nqk,nkd->nqd', score_grad, key_grp, preferred_element_type=jn...  155 us
  transfers between devices with their start and end apart: 10, of which 9 were waited for; matrix products, arithmetic and copies ran while one was open for 57% of the time, Pallas kernels for 0%

profile of v1, /device:TPU:0, one launch (start us, length us, event | category | flops | bytes accessed | tf_op | source)
XLA Modules:
  0.0 5214.7 jit_solution(4548712589432820216)
XLA Ops:
  17.9 106.0 %all-gather.7.cloned.1.call-done = bf16[4096,1024]{1,0:T(8,128)(2,1)} async-done(((bf16[2048,1024]{1,0:T(8,128)(2,1)}), bf16[4096,1024]{1,0:T(8,128)(2,1)}) %all-gather.7.cloned.1.call-update) | async-done | bytes 8388624 | tf_op jit(solution)/shard_map/all_gather | solution.py:225
  123.9 19.1 convolution_convert_fusion.2
  143.0 22.8 copy.94
  165.8 16.7 slice_bitcast_fusion
  182.5 961.9 %while.96 = (s32[]{:T(128)}, bf16[8,4096,64]{1,2,0:T(8,128)(2,1)}, f32[8,8,8,64]{3,2,1,0:T(8,128)}, f32[8,128]{1,0:T(8,128)}, bf16[8,4096,64]{2,1,0:T(8,128)(2,1...) while((s32[]{:T(128)}, bf16[8,4096,64]{1,2,0:T(8,128)(2,1)}, ...), condition=%wide.region_9.10_spmd, body=%wide.region_2.9_spmd.sunk | while | flops 275025280 | bytes 29968956 | solution.py:239
  200.6 93.2 %while.99 = (s32[]{:T(128)}, bf16[8,8,64,64]{3,2,1,0:T(8,128)(2,1)}, f32[8,8,64]{2,1,0:T(8,128)S(1)}, bf16[8,8,64,64]{3,2,1,0:T(8,128)(2,1)}, s32[8,8,8]{2,1,0:T...) while((s32[]{:T(128)}, bf16[8,8,64,64]{3,2,1,0:T(8,128)(2,1)}, f32[8,8,64]{2,1,0:T(8,128)S(1)}, ...), condition=%wide.region_6.6_spmd, body=%wide.region_3.5_spmd.sunk | while | flops 136580608 | bytes 10903893 | solution.py:94
  320.7 93.2 %while.99 = (s32[]{:T(128)}, bf16[8,8,64,64]{3,2,1,0:T(8,128)(2,1)}, f32[8,8,64]{2,1,0:T(8,128)S(1)}, bf16[8,8,64,64]{3,2,1,0:T(8,128)(2,1)}, s32[8,8,8]{2,1,0:T...) while((s32[]{:T(128)}, bf16[8,8,64,64]{3,2,1,0:T(8,128)(2,1)}, f32[8,8,64]{2,1,0:T(8,128)S(1)}, ...), condition=%wide.region_6.6_spmd, body=%wide.region_3.5_spmd.sunk | while | flops 136580608 | bytes 10903893 | solution.py:94
  441.0 93.2 %while.99 = (s32[]{:T(128)}, bf16[8,8,64,64]{3,2,1,0:T(8,128)(2,1)}, f32[8,8,64]{2,1,0:T(8,128)S(1)}, bf16[8,8,64,64]{3,2,1,0:T(8,128)(2,1)}, s32[8,8,8]{2,1,0:T...) while((s32[]{:T(128)}, bf16[8,8,64,64]{3,2,1,0:T(8,128)(2,1)}, f32[8,8,64]{2,1,0:T(8,128)S(1)}, ...), condition=%wide.region_6.6_spmd, body=%wide.region_3.5_spmd.sunk | while | flops 136580608 | bytes 10903893 | solution.py:94
  561.2 93.2 %while.99 = (s32[]{:T(128)}, bf16[8,8,64,64]{3,2,1,0:T(8,128)(2,1)}, f32[8,8,64]{2,1,0:T(8,128)S(1)}, bf16[8,8,64,64]{3,2,1,0:T(8,128)(2,1)}, s32[8,8,8]{2,1,0:T...) while((s32[]{:T(128)}, bf16[8,8,64,64]{3,2,1,0:T(8,128)(2,1)}, f32[8,8,64]{2,1,0:T(8,128)S(1)}, ...), condition=%wide.region_6.6_spmd, body=%wide.region_3.5_spmd.sunk | while | flops 136580608 | bytes 10903893 | solution.py:94
  681.3 93.2 %while.99 = (s32[]{:T(128)}, bf16[8,8,64,64]{3,2,1,0:T(8,128)(2,1)}, f32[8,8,64]{2,1,0:T(8,128)S(1)}, bf16[8,8,64,64]{3,2,1,0:T(8,128)(2,1)}, s32[8,8,8]{2,1,0:T...) while((s32[]{:T(128)}, bf16[8,8,64,64]{3,2,1,0:T(8,128)(2,1)}, f32[8,8,64]{2,1,0:T(8,128)S(1)}, ...), condition=%wide.region_6.6_spmd, body=%wide.region_3.5_spmd.sunk | while | flops 136580608 | bytes 10903893 | solution.py:94
  801.5 93.2 %while.99 = (s32[]{:T(128)}, bf16[8,8,64,64]{3,2,1,0:T(8,128)(2,1)}, f32[8,8,64]{2,1,0:T(8,128)S(1)}, bf16[8,8,64,64]{3,2,1,0:T(8,128)(2,1)}, s32[8,8,8]{2,1,0:T...) while((s32[]{:T(128)}, bf16[8,8,64,64]{3,2,1,0:T(8,128)(2,1)}, f32[8,8,64]{2,1,0:T(8,128)S(1)}, ...), condition=%wide.region_6.6_spmd, body=%wide.region_3.5_spmd.sunk | while | flops 136580608 | bytes 10903893 | solution.py:94
  921.7 93.2 %while.99 = (s32[]{:T(128)}, bf16[8,8,64,64]{3,2,1,0:T(8,128)(2,1)}, f32[8,8,64]{2,1,0:T(8,128)S(1)}, bf16[8,8,64,64]{3,2,1,0:T(8,128)(2,1)}, s32[8,8,8]{2,1,0:T...) while((s32[]{:T(128)}, bf16[8,8,64,64]{3,2,1,0:T(8,128)(2,1)}, f32[8,8,64]{2,1,0:T(8,128)S(1)}, ...), condition=%wide.region_6.6_spmd, body=%wide.region_3.5_spmd.sunk | while | flops 136580608 | bytes 10903893 | solution.py:94
  1042.0 93.2 %while.99 = (s32[]{:T(128)}, bf16[8,8,64,64]{3,2,1,0:T(8,128)(2,1)}, f32[8,8,64]{2,1,0:T(8,128)S(1)}, bf16[8,8,64,64]{3,2,1,0:T(8,128)(2,1)}, s32[8,8,8]{2,1,0:T...) while((s32[]{:T(128)}, bf16[8,8,64,64]{3,2,1,0:T(8,128)(2,1)}, f32[8,8,64]{2,1,0:T(8,128)S(1)}, ...), condition=%wide.region_6.6_spmd, body=%wide.region_3.5_spmd.sunk | while | flops 136580608 | bytes 10903893 | solution.py:94
  1144.5 10.6 convolution_convert_fusion.5
  1155.1 99.4 %reduce-scatter.5.cloned.1.call-done = bf16[2048,1024]{1,0:T(8,128)(2,1)} async-done(((bf16[4096,1024]{1,0:T(8,128)(2,1)}), bf16[2048,1024]{1,0:T(8,128)(2,1)}) %reduce-scatter.5.cloned.1.call-update) | async-done | bytes 4194320 | tf_op jit(solution)/shard_map/reduce_scatter | solution.py:247
  1267.0 103.5 %all-gather.9.cloned.1.call-done = bf16[4096,1024]{1,0:T(8,128)(2,1)} async-done(((bf16[2048,1024]{1,0:T(8,128)(2,1)}), bf16[4096,1024]{1,0:T(8,128)(2,1)}) %all-gather.9.cloned.1.call-update) | async-done | bytes 8388624 | tf_op jit(solution)/shard_map/all_gather | solution.py:256
  1370.5 34.5 multiply_convert_fusion.2
  1405.0 70.9 %all-gather.11.cloned.1.call-done = bf16[4096,1024]{1,0:T(8,128)(2,1)} async-done(((bf16[2048,1024]{1,0:T(8,128)(2,1)}), bf16[4096,1024]{1,0:T(8,128)(2,1)}) %all-gather.11.cloned.1.call-update) | async-done | bytes 8388624 | tf_op jit(solution)/shard_map/all_gather | solution.py:257
  1475.9 45.3 fusion.101
  1521.1 23.7 convolution_convert_fusion.3
  1545.0 99.4 %reduce-scatter.9.cloned.1.call-done = bf16[2048,1024]{1,0:T(8,128)(2,1)} async-done(((bf16[4096,1024]{1,0:T(8,128)(2,1)}), bf16[2048,1024]{1,0:T(8,128)(2,1)}) %reduce-scatter.9.cloned.1.call-update) | async-done | bytes 4194320 | tf_op jit(solution)/shard_map/reduce_scatter | solution.py:276
  1644.4 8.9 fusion.86
  1653.9 7.1 fusion.94
  1661.1 24.3 convolution_convert_fusion.8
  1685.4 23.7 convolution_convert_fusion.7
  1709.2 56.0 %all-gather.13.cloned.1.call-done = bf16[4096,1024]{1,0:T(8,128)(2,1)} async-done(((bf16[2048,1024]{1,0:T(8,128)(2,1)}), bf16[4096,1024]{1,0:T(8,128)(2,1)}) %all-gather.13.cloned.1.call-update) | async-done | bytes 8388624 | tf_op jit(solution)/shard_map/all_gather | solution.py:286
  1765.2 10.1 convolution_convert_fusion.6
  1775.3 8.3 copy.97
  1783.7 10.2 convolution_convert_fusion.9
  1793.9 2905.6 %while.98 = (s32[]{:T(128)}, bf16[8,4096,64]{1,2,0:T(8,128)(2,1)}, bf16[8,4096,64]{1,2,0:T(8,128)(2,1)}, bf16[8,4096,64]{1,2,0:T(8,128)(2,1)}, bf16[8,4096,64]{2...) while((s32[]{:T(128)}, bf16[8,4096,64]{1,2,0:T(8,128)(2,1)}, ...), condition=%wide.region_22.23_spmd, body=%wide.region_17.22_spmd.sunk | while | flops 983490496 | bytes 111270584 | solution.py:298
  1817.9 307.3 %while.100 = (s32[]{:T(128)}, f32[64,8192]{1,0:T(8,128)}, f32[8,8,64,64]{3,2,1,0:T(8,128)}, s32[8,8,8]{2,1,0:T(8,128)S(1)}, bf16[8,8,64,64]{3,2,1,0:T(8,128)(2,1...) while((s32[]{:T(128)}, f32[64,8192]{1,0:T(8,128)}, ...), condition=%wide.region_20.20_spmd.clone, body=%wide.region_18.19_spmd.clone.sunk | while | flops 642031104 | bytes 48511176 | solution.py:174
  1887.0 4.8 convolution_add_fusion.3
  1925.8 4.9 convolution_add_fusion.3
  1964.4 4.8 convolution_add_fusion.3
  2002.8 4.8 convolution_add_fusion.3
  2129.8 4.8 fusion.189
  2181.8 306.4 %while.100 = (s32[]{:T(128)}, f32[64,8192]{1,0:T(8,128)}, f32[8,8,64,64]{3,2,1,0:T(8,128)}, s32[8,8,8]{2,1,0:T(8,128)S(1)}, bf16[8,8,64,64]{3,2,1,0:T(8,128)(2,1...) while((s32[]{:T(128)}, f32[64,8192]{1,0:T(8,128)}, ...), condition=%wide.region_20.20_spmd.clone, body=%wide.region_18.19_spmd.clone.sunk | while | flops 642031104 | bytes 48511176 | solution.py:174
  2492.8 4.8 fusion.189
  2544.7 306.4 %while.100 = (s32[]{:T(128)}, f32[64,8192]{1,0:T(8,128)}, f32[8,8,64,64]{3,2,1,0:T(8,128)}, s32[8,8,8]{2,1,0:T(8,128)S(1)}, bf16[8,8,64,64]{3,2,1,0:T(8,128)(2,1...) while((s32[]{:T(128)}, f32[64,8192]{1,0:T(8,128)}, ...), condition=%wide.region_20.20_spmd.clone, body=%wide.region_18.19_spmd.clone.sunk | while | flops 642031104 | bytes 48511176 | solution.py:174
  2855.7 4.8 fusion.189
  2907.7 306.4 %while.100 = (s32[]{:T(128)}, f32[64,8192]{1,0:T(8,128)}, f32[8,8,64,64]{3,2,1,0:T(8,128)}, s32[8,8,8]{2,1,0:T(8,128)S(1)}, bf16[8,8,64,64]{3,2,1,0:T(8,128)(2,1...) while((s32[]{:T(128)}, f32[64,8192]{1,0:T(8,128)}, ...), condition=%wide.region_20.20_spmd.clone, body=%wide.region_18.19_spmd.clone.sunk | while | flops 642031104 | bytes 48511176 | solution.py:174
  3218.7 4.8 fusion.189
  3270.6 306.4 %while.100 = (s32[]{:T(128)}, f32[64,8192]{1,0:T(8,128)}, f32[8,8,64,64]{3,2,1,0:T(8,128)}, s32[8,8,8]{2,1,0:T(8,128)S(1)}, bf16[8,8,64,64]{3,2,1,0:T(8,128)(2,1...) while((s32[]{:T(128)}, f32[64,8192]{1,0:T(8,128)}, ...), condition=%wide.region_20.20_spmd.clone, body=%wide.region_18.19_spmd.clone.sunk | while | flops 642031104 | bytes 48511176 | solution.py:174
  3581.6 4.8 fusion.189
  3633.6 306.4 %while.100 = (s32[]{:T(128)}, f32[64,8192]{1,0:T(8,128)}, f32[8,8,64,64]{3,2,1,0:T(8,128)}, s32[8,8,8]{2,1,0:T(8,128)S(1)}, bf16[8,8,64,64]{3,2,1,0:T(8,128)(2,1...) while((s32[]{:T(128)}, f32[64,8192]{1,0:T(8,128)}, ...), condition=%wide.region_20.20_spmd.clone, body=%wide.region_18.19_spmd.clone.sunk | while | flops 642031104 | bytes 48511176 | solution.py:174
  3944.6 4.8 fusion.189
  3996.5 306.4 %while.100 = (s32[]{:T(128)}, f32[64,8192]{1,0:T(8,128)}, f32[8,8,64,64]{3,2,1,0:T(8,128)}, s32[8,8,8]{2,1,0:T(8,128)S(1)}, bf16[8,8,64,64]{3,2,1,0:T(8,128)(2,1...) while((s32[]{:T(128)}, f32[64,8192]{1,0:T(8,128)}, ...), condition=%wide.region_20.20_spmd.clone, body=%wide.region_18.19_spmd.clone.sunk | while | flops 642031104 | bytes 48511176 | solution.py:174
  4307.5 4.8 fusion.189
  4359.5 306.4 %while.100 = (s32[]{:T(128)}, f32[64,8192]{1,0:T(8,128)}, f32[8,8,64,64]{3,2,1,0:T(8,128)}, s32[8,8,8]{2,1,0:T(8,128)S(1)}, bf16[8,8,64,64]{3,2,1,0:T(8,128)(2,1...) while((s32[]{:T(128)}, f32[64,8192]{1,0:T(8,128)}, ...), condition=%wide.region_20.20_spmd.clone, body=%wide.region_18.19_spmd.clone.sunk | while | flops 642031104 | bytes 48511176 | solution.py:174
  4670.5 4.8 fusion.189
  4699.5 6.6 pad_maximum_fusion.6
  4710.7 17.6 bitcast_convert_fusion
  4728.3 23.4 convolution_convert_fusion.4
  4751.8 19.8 convert_bitcast_fusion.3
  4776.4 32.5 psum.69
  4809.4 6.9 convert_element_type.166
  4822.4 5.1 reduce-scatter.11.cloned.1.call-done
  4827.5 6.1 fusion.87
  4833.7 96.1 %reduce-scatter.7.cloned.1.call-done = bf16[2048,1024]{1,0:T(8,128)(2,1)} async-done(((bf16[4096,1024]{1,0:T(8,128)(2,1)}), bf16[2048,1024]{1,0:T(8,128)(2,1)}) %reduce-scatter.7.cloned.1.call-update) | async-done | bytes 4194320 | tf_op jit(solution)/shard_map/reduce_scatter | solution.py:261
  4929.8 17.7 fusion.80
  4947.5 43.1 all-reduce
  4990.7 188.7 %all-gather.15.cloned.1.call-done = bf16[48,1024,512]{2,1,0:T(8,128)(2,1)} async-done(((bf16[3,1024,512]{2,1,0:T(8,128)(2,1)}), bf16[48,1024,512]{2,1,0:T(8,128)(2,1)}) %all-gather.15.cloned.1.call-update) | async-done | bytes 50331664 | tf_op jit(solution)/shard_map/all_gather | solution.py:323
  5179.3 18.3 reduce_sum.195
  5202.3 5.4 copy.102
  (2686 shorter events, 3846.7 us)
Async XLA Ops:
  7.2 116.7 %copy-start = (bf16[3,1024,512]{2,1,0:T(8,128)(2,1)S(1)}, bf16[3,1024,512]{2,1,0:T(8,128)(2,1)}, u32[]{:S(2)}) copy-start(bf16[3,1024,512]{2,1,0:T(8,128)(2,1)} %param.33) | copy-start | bytes 9437188
  7.2 6.8 copy-start.34
  7.2 6.8 copy-start.39
  7.2 116.7 %all-gather.7.cloned.1.call-start = ((), (), s32[]{:S(2)}) async-start(), calls=%async_computation.4 | async-start | bytes 12582912 | tf_op jit(solution)/shard_map/all_gather | solution.py:225
  7.3 6.7 copy-start.5
  10.3 7.1 copy-start.38
  17.0 1237.5 %reduce-scatter.5.cloned.1.call-start = ((), (), s32[]{:S(2)}) async-start(), calls=%async_computation.5 | async-start | bytes 12582912 | tf_op jit(solution)/shard_map/reduce_scatter | solution.py:247
  1144.4 10.6 copy-start.15
  1155.0 107.8 %copy-start.31 = (f32[1024]{0:T(1024)S(1)}, f32[1024]{0:T(1024)}, u32[]{:S(2)}) copy-start(f32[1024]{0:T(1024)} %param.35) | copy-start | bytes 12292
  1155.0 107.8 %copy-start.40 = (f32[1024]{0:T(1024)S(1)}, f32[1024]{0:T(1024)}, u32[]{:S(2)}) copy-start(f32[1024]{0:T(1024)} %param.36) | copy-start | bytes 12292
  1155.1 215.4 %all-gather.9.cloned.1.call-start = ((), (), s32[]{:S(2)}) async-start(), calls=%async_computation.6 | async-start | bytes 12582912 | tf_op jit(solution)/shard_map/all_gather | solution.py:256
  1254.5 4.8 copy-start.6
  1254.5 5.9 copy-start.10
  1262.9 107.6 %copy-start.43 = (f32[2048]{0:T(1024)S(1)}, f32[2048]{0:T(1024)}, u32[]{:S(2)}) copy-start(f32[2048]{0:T(1024)} %param.38) | copy-start | bytes 24580
  1266.3 209.5 %all-gather.11.cloned.1.call-start = ((), (), s32[]{:S(2)}) async-start(), calls=%async_computation.8 | async-start | bytes 12582912 | tf_op jit(solution)/shard_map/all_gather | solution.py:257
  1266.9 377.5 %reduce-scatter.9.cloned.1.call-start = ((), (), s32[]{:S(2)}) async-start(), calls=%async_computation.9 | async-start | bytes 12582912 | tf_op jit(solution)/shard_map/reduce_scatter | solution.py:276
  1544.9 99.5 %copy-start.18 = (f32[2048]{0:T(1024)S(1)}, f32[2048]{0:T(1024)}, u32[]{:S(2)}) copy-start(f32[2048]{0:T(1024)} %copy-done.17) | copy-start | bytes 24580
  1544.9 99.5 %copy-start.23 = (f32[2048]{0:T(1024)S(1)}, f32[2048]{0:T(1024)}, u32[]{:S(2)}) copy-start(f32[2048]{0:T(1024)} %copy-done.22) | copy-start | bytes 24580
  1544.9 99.5 %copy-start.32 = (f32[1024]{0:T(1024)S(1)}, f32[1024]{0:T(1024)}, u32[]{:S(2)}) copy-start(f32[1024]{0:T(1024)} %param.35) | copy-start | bytes 12292
  1544.9 220.3 %all-gather.13.cloned.1.call-start = ((), (), s32[]{:S(2)}) async-start(), calls=%async_computation.10 | async-start | bytes 12582912 | tf_op jit(solution)/shard_map/all_gather | solution.py:286
  1644.4 9.5 copy-start.7
  1644.4 9.5 copy-start.11
  1644.4 9.5 copy-start.12
  1661.1 3148.4 %all-reduce.4.cloned.1.call-start = ((), (), s32[]{:S(2)}) async-start(), calls=%async_computation.13 | async-start | bytes 18874368 | tf_op jit(solution)/shard_map/psum | solution.py:324
  1793.9 3033.7 %reduce-scatter.11.cloned.1.call-start = ((), (), s32[]{:S(2)}) async-start(), calls=%async_computation.11 | async-start | bytes 12582912 | tf_op jit(solution)/shard_map/reduce_scatter | solution.py:309
  1826.6 3.3 copy-start.2
  1903.1 3.3 copy-start.2
  2018.7 3.3 copy-start.2
  2228.2 3.3 copy-start.2
  2266.6 3.3 copy-start.2
  2381.8 3.3 copy-start.2
  2553.5 3.3 copy-start.2
  2591.2 3.3 copy-start.2
  2629.6 3.3 copy-start.2
  2744.7 3.3 copy-start.2
  2954.2 3.3 copy-start.2
  2992.5 3.3 copy-start.2
  3107.7 3.3 copy-start.2
  3317.1 3.3 copy-start.2
  3355.5 3.3 copy-start.2
  3470.6 3.3 copy-start.2
  3642.3 3.3 copy-start.2
  3680.0 3.3 copy-start.2
  3718.4 3.3 copy-start.2
  3833.5 3.3 copy-start.2
  4043.0 3.3 copy-start.2
  4406.0 3.3 copy-start.2
  4706.1 4.5 copy-start.13
  4728.3 201.5 %reduce-scatter.7.cloned.1.call-start = ((), (), s32[]{:S(2)}) async-start(), calls=%async_computation.7 | async-start | bytes 12582912 | tf_op jit(solution)/shard_map/reduce_scatter | solution.py:261
  4751.8 427.6 %all-gather.15.cloned.1.call-start = ((), (), s32[]{:S(2)}) async-start(), calls=%async_computation.12 | async-start | bytes 53477376 | tf_op jit(solution)/shard_map/all_gather | solution.py:323
  4771.6 4.7 copy-start.42
  4809.4 6.9 copy-start.14
  4816.3 4.5 copy-start.16
  4816.3 11.2 copy-start.21
  4816.3 11.2 copy-start.26
  4816.3 11.2 copy-start.35
  4820.8 109.0 %copy-start.19 = (f32[2048]{0:T(1024)S(1)}, f32[2048]{0:T(1024)}, u32[]{:S(2)}) copy-start(f32[2048]{0:T(1024)} %copy-done.17) | copy-start | bytes 24580
  4820.8 109.0 %copy-start.24 = (f32[2048]{0:T(1024)S(1)}, f32[2048]{0:T(1024)}, u32[]{:S(2)}) copy-start(f32[2048]{0:T(1024)} %copy-done.22) | copy-start | bytes 24580
  4820.8 109.0 %copy-start.28 = (f32[2048]{0:T(1024)S(1)}, f32[2048]{0:T(1024)}, u32[]{:S(2)}) copy-start(f32[2048]{0:T(1024)} %copy-done.27) | copy-start | bytes 24580
  4820.8 109.0 %copy-start.30 = (f32[2048]{0:T(1024)S(1)}, f32[2048]{0:T(1024)}, u32[]{:S(2)}) copy-start(f32[2048]{0:T(1024)} %copy-done.29) | copy-start | bytes 24580
  4820.8 109.0 %copy-start.33 = (f32[1024]{0:T(1024)S(1)}, f32[1024]{0:T(1024)}, u32[]{:S(2)}) copy-start(f32[1024]{0:T(1024)} %param.35) | copy-start | bytes 12292
  4820.8 109.0 %copy-start.41 = (f32[1024]{0:T(1024)S(1)}, f32[1024]{0:T(1024)}, u32[]{:S(2)}) copy-start(f32[1024]{0:T(1024)} %param.40) | copy-start | bytes 12292
  4833.7 113.9 %copy-start.36 = (f32[1024]{0:T(1024)S(1)}, f32[1024]{0:T(1024)}, u32[]{:S(2)}) copy-start(f32[1024]{0:T(1024)} %get-tuple-element.510) | copy-start | bytes 12292
  4833.7 113.9 %copy-start.37 = (f32[1024]{0:T(1024)S(1)}, f32[1024]{0:T(1024)}, u32[]{:S(2)}) copy-start(f32[1024]{0:T(1024)} %get-tuple-element.516) | copy-start | bytes 12292
  (200 other events, 284.0 us)
Sparse Core Ops, SparseCore 0:
  17.1 106.6 all-gather.6
  1155.2 99.3 reduce-scatter.4
  1266.5 103.9 all-gather.8
  1371.9 103.9 all-gather.10
  1545.0 99.3 reduce-scatter.8
  1661.2 103.9 all-gather.12
  1794.0 184.7 all-reduce.3
  4728.4 99.0 reduce-scatter.10
  4830.4 99.3 reduce-scatter.6
  4931.2 248.1 all-gather.14
